TPU v7x, 32 devices: a whole 2x2x4 slice. The times are simulated.
32 devices in a mesh: row: 8 (over y, x, core), col: 4 (over z).
Axes of the slice: x: 2, y: 2, z: 4, core: 2. Of those that a mesh axis runs over, the one named last changes fastest.
Arguments:
- density_start: float32 [512, 512], P('row', 'col'), may hold values from -0.5 to 1, as said below
- branches: int32 [6], replicated, may hold values from 0 to 1, as said below
Outputs:
- density: float32 [512, 512], P('row', 'col')
- occupations: float32 [6, 2], replicated
Inputs may be any that keep to these rules, and one draw needn't show every extreme that they name: density_start is symmetric with eigenvalues inside 0 to 1. `branches`: each entry is 0 or 1, and exactly 3 entries are 1.
All inputs are finite; a program needn't handle non-finite values.
Results may differ from a plain program's by a relative error of at most 0.0025.
Values may be sent and summed in bfloat16 or wider, within the bound.
A program may use at most 64 MiB of HBM per device.

v0:
```python
import jax
import jax.numpy as jnp
from jax import lax
from jax.sharding import PartitionSpec as P

ITERS = 6


def taken_in(shard, axis, dim, absorb, state):
    everything = jax.tree.map(lambda a: lax.all_gather(a, axis, axis=dim, tiled=True), shard)
    return absorb(state, everything, jnp.int32(0))


def local_trace(matrix_block, diagonal_mask):
    return jnp.sum(matrix_block * diagonal_mask)


def body(density_start, branches):
    rows_here, cols_here = density_start.shape
    row_first = lax.axis_index("row") * rows_here
    col_first = lax.axis_index("col") * cols_here
    row_ids = row_first + lax.broadcasted_iota(jnp.int32, (rows_here, cols_here), 0)
    col_ids = col_first + lax.broadcasted_iota(jnp.int32, (rows_here, cols_here), 1)
    diagonal_mask = (row_ids == col_ids).astype(jnp.float32)
    size_total = cols_here * lax.axis_size("col")
    density = density_start
    records = []
    for iteration in range(ITERS):
        narrow = density.astype(jnp.bfloat16)
        empty = jnp.zeros((rows_here, cols_here), jnp.float32)
        plain_local = local_trace(density, diagonal_mask)
        row_panel = lax.all_gather(narrow, "col", axis=1, tiled=True)

        def add_rows(accumulated, shard_piece, offset):
            panel_part = lax.dynamic_slice_in_dim(row_panel, offset, shard_piece.shape[0], 1)
            return accumulated + jnp.dot(
                panel_part, shard_piece, preferred_element_type=jnp.float32
            )

        square = taken_in(narrow, "row", 0, add_rows, empty)
        square_local = local_trace(square, diagonal_mask)
        branch_now = branches[iteration]
        records.append(jnp.stack([plain_local, square_local]))
        density = jnp.where(branch_now == 1, 2.0 * density - square, square)
    stacked = jnp.stack(records)
    stacked = lax.psum(stacked, ("row", "col"))
    occupations = stacked / size_total
    return (density, occupations)


def solution(mesh):
    in_specs = (P("row", "col"), P())
    out_specs = (P("row", "col"), P())
    return jax.shard_map(body, mesh=mesh, in_specs=in_specs, out_specs=out_specs, check_vma=False)
```

profile of v0, /device:TPU:0, one launch (start us, length us, event | category | flops | bytes accessed | tf_op | source)
XLA Modules:
  0.0 182.0 jit_solution(16147823306401190443)
XLA Ops:
  0.7 1.6 fusion.17
  6.1 13.7 %all_gather.36 = bf16[64,512]{1,0:T(8,128)(2,1)S(1)} all-gather(bf16[64,128]{1,0:T(8,128)(2,1)S(1)} %convert_element_type.19), channel_id=1, replica_groups=mesh['row'=8,'col'=4] {'col'}, dimensions={1}, use_global_device_ids=true | all-gather | bytes 81920 | tf_op jit(solution)/shard_map/all_gather | solution.py:32
  19.8 9.2 %all_gather.37 = bf16[512,128]{1,0:T(8,128)(2,1)S(1)} all-gather(bf16[64,128]{1,0:T(8,128)(2,1)S(1)} %convert_element_type.19), channel_id=1, replica_groups=mesh['row'=8,'col'=4] {'row'}, dimensions={0}, use_global_device_ids=true | all-gather | bytes 147456 | tf_op jit(solution)/shard_map/all_gather | solution.py:10
  29.0 0.2 fusion.16
  29.2 12.0 %all_gather.38 = bf16[64,512]{1,0:T(8,128)(2,1)S(1)} all-gather(bf16[64,128]{1,0:T(8,128)(2,1)S(1)} %get-tuple-element.24), channel_id=1, replica_groups=mesh['row'=8,'col'=4] {'col'}, dimensions={1}, use_global_device_ids=true | all-gather | bytes 81920 | tf_op jit(solution)/shard_map/all_gather | solution.py:32
  41.2 9.2 %all_gather.39 = bf16[512,128]{1,0:T(8,128)(2,1)S(1)} all-gather(bf16[64,128]{1,0:T(8,128)(2,1)S(1)} %get-tuple-element.24), channel_id=1, replica_groups=mesh['row'=8,'col'=4] {'row'}, dimensions={0}, use_global_device_ids=true | all-gather | bytes 147456 | tf_op jit(solution)/shard_map/all_gather | solution.py:10
  50.5 12.0 %all_gather.40 = bf16[64,512]{1,0:T(8,128)(2,1)S(1)} all-gather(bf16[64,128]{1,0:T(8,128)(2,1)S(1)} %get-tuple-element.22), channel_id=1, replica_groups=mesh['row'=8,'col'=4] {'col'}, dimensions={1}, use_global_device_ids=true | all-gather | bytes 81920 | tf_op jit(solution)/shard_map/all_gather | solution.py:32
  62.5 8.2 %all_gather.41 = bf16[512,128]{1,0:T(8,128)(2,1)S(1)} all-gather(bf16[64,128]{1,0:T(8,128)(2,1)S(1)} %get-tuple-element.22), channel_id=1, replica_groups=mesh['row'=8,'col'=4] {'row'}, dimensions={0}, use_global_device_ids=true | all-gather | bytes 147456 | tf_op jit(solution)/shard_map/all_gather | solution.py:10
  70.9 12.0 %all_gather.42 = bf16[64,512]{1,0:T(8,128)(2,1)S(1)} all-gather(bf16[64,128]{1,0:T(8,128)(2,1)S(1)} %get-tuple-element.20), channel_id=1, replica_groups=mesh['row'=8,'col'=4] {'col'}, dimensions={1}, use_global_device_ids=true | all-gather | bytes 81920 | tf_op jit(solution)/shard_map/all_gather | solution.py:32
  82.9 9.2 %all_gather.43 = bf16[512,128]{1,0:T(8,128)(2,1)S(1)} all-gather(bf16[64,128]{1,0:T(8,128)(2,1)S(1)} %get-tuple-element.20), channel_id=1, replica_groups=mesh['row'=8,'col'=4] {'row'}, dimensions={0}, use_global_device_ids=true | all-gather | bytes 147456 | tf_op jit(solution)/shard_map/all_gather | solution.py:10
  92.1 0.2 fusion.13
  92.2 12.0 %all_gather.44 = bf16[64,512]{1,0:T(8,128)(2,1)S(1)} all-gather(bf16[64,128]{1,0:T(8,128)(2,1)S(1)} %get-tuple-element.18), channel_id=1, replica_groups=mesh['row'=8,'col'=4] {'col'}, dimensions={1}, use_global_device_ids=true | all-gather | bytes 81920 | tf_op jit(solution)/shard_map/all_gather | solution.py:32
  104.2 8.2 %all_gather.45 = bf16[512,128]{1,0:T(8,128)(2,1)S(1)} all-gather(bf16[64,128]{1,0:T(8,128)(2,1)S(1)} %get-tuple-element.18), channel_id=1, replica_groups=mesh['row'=8,'col'=4] {'row'}, dimensions={0}, use_global_device_ids=true | all-gather | bytes 147456 | tf_op jit(solution)/shard_map/all_gather | solution.py:10
  112.6 12.0 %all_gather.46 = bf16[64,512]{1,0:T(8,128)(2,1)S(1)} all-gather(bf16[64,128]{1,0:T(8,128)(2,1)S(1)} %get-tuple-element.16), channel_id=1, replica_groups=mesh['row'=8,'col'=4] {'col'}, dimensions={1}, use_global_device_ids=true | all-gather | bytes 81920 | tf_op jit(solution)/shard_map/all_gather | solution.py:32
  124.6 9.2 %all_gather.47 = bf16[512,128]{1,0:T(8,128)(2,1)S(1)} all-gather(bf16[64,128]{1,0:T(8,128)(2,1)S(1)} %get-tuple-element.16), channel_id=1, replica_groups=mesh['row'=8,'col'=4] {'row'}, dimensions={0}, use_global_device_ids=true | all-gather | bytes 147456 | tf_op jit(solution)/shard_map/all_gather | solution.py:10
  133.8 1.5 fusion.10
  135.2 1.3 maximum_bitcast_fusion.5
  136.6 1.3 maximum_bitcast_fusion.4
  138.1 1.3 maximum_bitcast_fusion.3
  139.4 1.3 maximum_bitcast_fusion.2
  140.9 1.3 maximum_bitcast_fusion.1
  142.3 1.3 maximum_bitcast_fusion
  143.8 37.7 %psum.7 = f32[6,2]{0,1:T(2,128)S(1)} all-reduce(f32[6,2]{0,1:T(2,128)S(1)} %stack.99), channel_id=1, replica_groups=mesh['row'=8,'col'=4] {'row','col'}, use_global_device_ids=true, to_apply=%region_12.13 | all-reduce | flops 12 | bytes 96 | tf_op jit(solution)/shard_map/psum | solution.py:46
  181.5 0.6 broadcast_multiply_fusion
  (15 shorter events, 1.2 us)
Async XLA Ops:
  0.6 5.5 %copy-start = (f32[64,128]{1,0:T(8,128)S(1)}, f32[64,128]{1,0:T(8,128)}, u32[]{:S(2)}) copy-start(f32[64,128]{1,0:T(8,128)} %param.2) | copy-start | bytes 98308
where the time goes:
time: 183 us; the launch traced here: 182 us
  blocking collectives  165 us (90%)
  other arithmetic  8.46 us (5%)
  between operations  4.56 us (2%)
  matrix products  2.26 us (1%)
  local copies, waits for them, and re-layouts  2.23 us (1%)
    all_gather x6, blocking collectives, body(): row_panel = lax.all_gather(narrow, 'col', axis=1, tiled=True)  73.7 us
    all_gather x6, blocking collectives, taken_in(): lax.all_gather(a, axis, axis=dim, tiled=True)  53.2 us
    psum x1, blocking collectives, body(): stacked = lax.psum(stacked, ('row', 'col'))  37.7 us
    another operation x6, other arithmetic, body(): stacked = jnp.stack(records)  7.88 us

commit v1 on v0

--- a/solution.py
+++ b/solution.py
@@ -43,7 +43,7 @@
         records.append(jnp.stack([plain_local, square_local]))
         density = jnp.where(branch_now == 1, 2.0 * density - square, square)
     stacked = jnp.stack(records)
-    stacked = lax.psum(stacked, ("row", "col"))
+    stacked = jnp.sum(lax.all_gather(stacked, ("row", "col")), axis=0)
     occupations = stacked / size_total
     return (density, occupations)
 

time: 183 us -> 209 us (1.14)
  blocking collectives: 165 us -> 191 us
    all_gather x0 -> x1, blocking collectives: none -> 64.2 us  [body(): stacked = jnp.sum(lax.all_gather(stacked, ('row', 'col')), axis=0)]
    psum x1 -> x0, blocking collectives: 37.7 us -> none  [body(): stacked = lax.psum(stacked, ('row', 'col'))]
where the time goes in v1:
time: 209 us
  blocking collectives  191 us (91%)
  other arithmetic  8.5 us (4%)
  between operations  4.56 us (2%)
  matrix products  2.26 us (1%)
  local copies, waits for them, and re-layouts  2.23 us (1%)
    all_gather x6, blocking collectives, body(): row_panel = lax.all_gather(narrow, 'col', axis=1, tiled=True)  73.7 us
    all_gather x1, blocking collectives, body(): stacked = jnp.sum(lax.all_gather(stacked, ('row', 'col')), axis=0)  64.2 us
    all_gather x6, blocking collectives, taken_in(): lax.all_gather(a, axis, axis=dim, tiled=True)  53.2 us
    another operation x6, other arithmetic, body(): stacked = jnp.stack(records)  7.88 us

profile of v1, /device:TPU:0, one launch (start us, length us, event | category | flops | bytes accessed | tf_op | source)
XLA Modules:
  0.0 208.6 jit_solution(3072413517566236486)
XLA Ops:
  0.7 1.6 fusion.17
  6.1 13.7 %all_gather.42 = bf16[64,512]{1,0:T(8,128)(2,1)S(1)} all-gather(bf16[64,128]{1,0:T(8,128)(2,1)S(1)} %convert_element_type.19), channel_id=1, replica_groups=mesh['row'=8,'col'=4] {'col'}, dimensions={1}, use_global_device_ids=true | all-gather | bytes 81920 | tf_op jit(solution)/shard_map/all_gather | solution.py:32
  19.8 9.2 %all_gather.43 = bf16[512,128]{1,0:T(8,128)(2,1)S(1)} all-gather(bf16[64,128]{1,0:T(8,128)(2,1)S(1)} %convert_element_type.19), channel_id=1, replica_groups=mesh['row'=8,'col'=4] {'row'}, dimensions={0}, use_global_device_ids=true | all-gather | bytes 147456 | tf_op jit(solution)/shard_map/all_gather | solution.py:10
  29.0 0.2 fusion.16
  29.2 12.0 %all_gather.44 = bf16[64,512]{1,0:T(8,128)(2,1)S(1)} all-gather(bf16[64,128]{1,0:T(8,128)(2,1)S(1)} %get-tuple-element.22), channel_id=1, replica_groups=mesh['row'=8,'col'=4] {'col'}, dimensions={1}, use_global_device_ids=true | all-gather | bytes 81920 | tf_op jit(solution)/shard_map/all_gather | solution.py:32
  41.2 9.2 %all_gather.45 = bf16[512,128]{1,0:T(8,128)(2,1)S(1)} all-gather(bf16[64,128]{1,0:T(8,128)(2,1)S(1)} %get-tuple-element.22), channel_id=1, replica_groups=mesh['row'=8,'col'=4] {'row'}, dimensions={0}, use_global_device_ids=true | all-gather | bytes 147456 | tf_op jit(solution)/shard_map/all_gather | solution.py:10
  50.5 12.0 %all_gather.46 = bf16[64,512]{1,0:T(8,128)(2,1)S(1)} all-gather(bf16[64,128]{1,0:T(8,128)(2,1)S(1)} %get-tuple-element.20), channel_id=1, replica_groups=mesh['row'=8,'col'=4] {'col'}, dimensions={1}, use_global_device_ids=true | all-gather | bytes 81920 | tf_op jit(solution)/shard_map/all_gather | solution.py:32
  62.5 8.2 %all_gather.47 = bf16[512,128]{1,0:T(8,128)(2,1)S(1)} all-gather(bf16[64,128]{1,0:T(8,128)(2,1)S(1)} %get-tuple-element.20), channel_id=1, replica_groups=mesh['row'=8,'col'=4] {'row'}, dimensions={0}, use_global_device_ids=true | all-gather | bytes 147456 | tf_op jit(solution)/shard_map/all_gather | solution.py:10
  70.9 12.0 %all_gather.48 = bf16[64,512]{1,0:T(8,128)(2,1)S(1)} all-gather(bf16[64,128]{1,0:T(8,128)(2,1)S(1)} %get-tuple-element.18), channel_id=1, replica_groups=mesh['row'=8,'col'=4] {'col'}, dimensions={1}, use_global_device_ids=true | all-gather | bytes 81920 | tf_op jit(solution)/shard_map/all_gather | solution.py:32
  82.9 9.2 %all_gather.49 = bf16[512,128]{1,0:T(8,128)(2,1)S(1)} all-gather(bf16[64,128]{1,0:T(8,128)(2,1)S(1)} %get-tuple-element.18), channel_id=1, replica_groups=mesh['row'=8,'col'=4] {'row'}, dimensions={0}, use_global_device_ids=true | all-gather | bytes 147456 | tf_op jit(solution)/shard_map/all_gather | solution.py:10
  92.1 0.2 fusion.13
  92.2 12.0 %all_gather.50 = bf16[64,512]{1,0:T(8,128)(2,1)S(1)} all-gather(bf16[64,128]{1,0:T(8,128)(2,1)S(1)} %get-tuple-element.16), channel_id=1, replica_groups=mesh['row'=8,'col'=4] {'col'}, dimensions={1}, use_global_device_ids=true | all-gather | bytes 81920 | tf_op jit(solution)/shard_map/all_gather | solution.py:32
  104.2 8.2 %all_gather.51 = bf16[512,128]{1,0:T(8,128)(2,1)S(1)} all-gather(bf16[64,128]{1,0:T(8,128)(2,1)S(1)} %get-tuple-element.16), channel_id=1, replica_groups=mesh['row'=8,'col'=4] {'row'}, dimensions={0}, use_global_device_ids=true | all-gather | bytes 147456 | tf_op jit(solution)/shard_map/all_gather | solution.py:10
  112.6 12.0 %all_gather.52 = bf16[64,512]{1,0:T(8,128)(2,1)S(1)} all-gather(bf16[64,128]{1,0:T(8,128)(2,1)S(1)} %get-tuple-element.14), channel_id=1, replica_groups=mesh['row'=8,'col'=4] {'col'}, dimensions={1}, use_global_device_ids=true | all-gather | bytes 81920 | tf_op jit(solution)/shard_map/all_gather | solution.py:32
  124.6 9.2 %all_gather.53 = bf16[512,128]{1,0:T(8,128)(2,1)S(1)} all-gather(bf16[64,128]{1,0:T(8,128)(2,1)S(1)} %get-tuple-element.14), channel_id=1, replica_groups=mesh['row'=8,'col'=4] {'row'}, dimensions={0}, use_global_device_ids=true | all-gather | bytes 147456 | tf_op jit(solution)/shard_map/all_gather | solution.py:10
  133.8 1.5 fusion.10
  135.2 1.3 maximum_bitcast_fusion.5
  136.6 1.3 maximum_bitcast_fusion.4
  138.1 1.3 maximum_bitcast_fusion.3
  139.4 1.3 maximum_bitcast_fusion.2
  140.9 1.3 maximum_bitcast_fusion.1
  142.3 1.3 maximum_bitcast_fusion
  143.8 64.2 %all-gather.1 = f32[32,6,2]{1,2,0:T(2,128)S(1)} all-gather(f32[1,6,2]{1,2,0:T(2,128)S(1)} %bitcast.43), channel_id=2, replica_groups=mesh['row'=8,'col'=4] {'row','col'}, dimensions={0}, use_global_device_ids=true | all-gather | bytes 1584 | tf_op jit(solution)/shard_map/all_gather | solution.py:46
  208.0 0.6 broadcast_multiply_fusion
  (16 shorter events, 1.2 us)
Async XLA Ops:
  0.6 5.5 %copy-start = (f32[64,128]{1,0:T(8,128)S(1)}, f32[64,128]{1,0:T(8,128)}, u32[]{:S(2)}) copy-start(f32[64,128]{1,0:T(8,128)} %param.2) | copy-start | bytes 98308
